TPU v7x, 32 devices: a whole 2x2x4 slice. The times are simulated.
32 devices in a mesh: seg: 4 (over y, core), vid: 4 (over z), tp: 2 (over x).
Axes of the slice: x: 2, y: 2, z: 4, core: 2. Of those that a mesh axis runs over, the one named last changes fastest.
Arguments:
- tokens: bfloat16 [4, 2048, 2048], P('vid', 'seg', 'tp'), may hold values from -400 to 400
- key_weight: bfloat16 [2048, 2048], P('vid', 'tp'), may hold values from -0.125 to 0.125
- query_weight: bfloat16 [2048, 2048], P('vid', 'tp'), may hold values from -0.125 to 0.125
- latent_queries: bfloat16 [128, 2048], P(None, 'tp'), may hold values from -400 to 400
- init_memory: float32 [4, 128, 2048], P('vid', None, 'tp'), may hold values from -6 to 6
- forget: float32 [4, 4, 2048], P('vid', 'seg', 'tp'), may hold values from 0 to 1
Outputs:
- mixed: bfloat16 [4, 2048, 2048], P('vid', 'seg', 'tp')
- memory: float32 [4, 512, 2048], P('vid', 'seg', 'tp')
All inputs are finite; a program needn't handle non-finite values.
Results may differ from a plain program's by a relative error of at most 0.015.
The roundings to bfloat16 on the way count: a program that leaves them out, or rounds other values in their place, can miss the bound.
Values may be sent and summed in bfloat16 or wider, within the bound.
A program may use at most 64 MiB of HBM per device.

v0:
```python
import jax
import jax.numpy as jnp
from jax import lax
from jax.sharding import PartitionSpec as P

HEAD = 128


def from_behind(block, axis, distance):
    devices = range(lax.axis_size(axis))
    route = [(i - distance, i) for i in devices if i - distance in devices]
    return lax.ppermute(block, axis, route)


def trailing_softmax(scores):
    top = jnp.max(scores, axis=-1, keepdims=True)
    expo = jnp.exp(scores - top)
    return expo / jnp.sum(expo, axis=-1, keepdims=True)


def add_rows(left, piece):
    return jnp.dot(left, piece, preferred_element_type=jnp.float32)


def shards(tokens, key_weight, query_weight, latent_queries, init_memory, forget):
    local = tokens[0]
    width = local.shape[1]
    heads = width // HEAD
    latents = latent_queries.shape[0]
    whole = lax.all_gather(local, "tp", axis=1, tiled=True)

    def add_one(piece):
        return add_rows(whole, piece)

    keys_full = add_one(lax.all_gather(key_weight, "vid", axis=0, tiled=True))
    queries_full = add_one(lax.all_gather(query_weight, "vid", axis=0, tiled=True))
    scale = 1.0 / jnp.sqrt(jnp.float32(HEAD))
    keys = keys_full.astype(jnp.bfloat16).reshape(-1, heads, HEAD)
    queries = queries_full.astype(jnp.bfloat16).reshape(-1, heads, HEAD)
    values = local.reshape(-1, heads, HEAD)
    latent = latent_queries.reshape(latents, heads, HEAD)
    scores = jnp.einsum("mhe,the->hmt", latent, keys, preferred_element_type=jnp.float32) * scale
    weight_params = trailing_softmax(scores).astype(jnp.bfloat16)
    update = jnp.einsum(
        "hmt,the->mhe", weight_params, values, preferred_element_type=jnp.float32
    ).reshape(latents, width)
    retain = forget[0]
    initial_memory = init_memory[0]
    first = lax.axis_index("seg") == 0

    def turn(step, memory_now):
        received = from_behind(retain * memory_now + update, "seg", 1)
        return jnp.where(first, initial_memory, received)

    memory_in = lax.fori_loop(0, lax.axis_size("seg") - 1, turn, initial_memory)
    memory_out = retain * memory_in + update
    grouped = memory_in.reshape(latents, heads, HEAD)
    normed = grouped * lax.rsqrt(jnp.mean(grouped * grouped, axis=-1, keepdims=True) + 1e-06)
    read_scores = (
        jnp.einsum(
            "the,mhe->htm", queries, normed.astype(jnp.bfloat16), preferred_element_type=jnp.float32
        )
        * scale
    )
    read_weights = trailing_softmax(read_scores).astype(jnp.bfloat16)
    read = jnp.einsum(
        "htm,mhe->the",
        read_weights,
        grouped.astype(jnp.bfloat16),
        preferred_element_type=jnp.float32,
    )
    mixed = (local.astype(jnp.float32) + read.reshape(-1, width)).astype(jnp.bfloat16)
    return (mixed[None], memory_out[None])


def solution(mesh):
    placed = (
        P("vid", "seg", "tp"),
        P("vid", "tp"),
        P("vid", "tp"),
        P(None, "tp"),
        P("vid", None, "tp"),
        P("vid", "seg", "tp"),
    )
    return jax.shard_map(
        shards,
        mesh=mesh,
        in_specs=placed,
        out_specs=(P("vid", "seg", "tp"), P("vid", "seg", "tp")),
        check_vma=False,
    )
```

profile of v0, /device:TPU:6, one launch (start us, length us, event | category | flops | bytes accessed | tf_op | source)
XLA Modules:
  0.0 239.0 jit_solution(8553449657173419167)
XLA Ops:
  7.2 0.0 copy-start
  7.2 0.0 copy-start.2
  7.2 0.0 all-gather.9.cloned.1.call-start
  7.2 0.7 all-gather.9.cloned.1.call-update
  7.9 0.0 copy-start.1
  7.9 0.0 all-gather.5.cloned.1.call-start
  8.0 0.7 all-gather.5.cloned.1.call-update
  8.7 0.0 all-gather.7.cloned.1.call-start
  8.7 0.7 all-gather.7.cloned.1.call-update
  9.4 0.0 copy-done.2
  9.4 1.3 copy.45
  10.8 0.0 copy-done.1
  10.8 32.1 %all-gather.9.cloned.1.call-done = bf16[1,512,2048]{2,1,0:T(8,128)(2,1)} async-done(((bf16[1,512,1024]{2,1,0:T(8,128)(2,1)}), bf16[1,512,2048]{2,1,0:T(8,128)(2,1)}) %all-gather.9.cloned.1.call-update) | async-done | bytes 2097168 | tf_op jit(solution)/shard_map/all_gather | solution.py:30
  42.9 83.3 %all-gather.5.cloned.1.call-done = bf16[2048,1024]{1,0:T(8,128)(2,1)} async-done(((bf16[512,1024]{1,0:T(8,128)(2,1)}), bf16[2048,1024]{1,0:T(8,128)(2,1)}) %all-gather.5.cloned.1.call-update) | async-done | bytes 4194320 | tf_op jit(solution)/shard_map/all_gather | solution.py:35
  126.2 5.2 %fusion.21 = bf16[64,8,8,128]{3,2,1,0:T(8,128)(2,1)S(1)} fusion(bf16[2048,1024]{1,0:T(8,128)(2,1)} %all-gather.5.cloned.1.call-done, bf16[1,512,2048]{2,1,0:T(8,128)(2,1)} %all-gather.9.cloned.1.call-done), kind=kOutput, calls=%fused_computation.22 | convolution fusion | flops 2148007936 | bytes 7340032 | tf_op jit(solution)/shard_map/dot_general | solution.py:22
  131.3 0.0 copy-done
  131.4 0.4 fusion.27
  131.8 0.6 fusion.62
  132.4 0.0 copy-start.4
  132.4 3.1 %fusion.33 = f32[8,128,128]{1,2,0:T(8,128)} fusion(bf16[512,8,128]{0,2,1:T(8,128)(2,1)} %bitcast.82, f32[8,128]{1,0:T(8,128)S(1)} %fusion.62, f32[8,512,128]{2,1,0:T(8,128)S(1)} %fusion.27), kind=kOutput, calls=%fused_computation.32 | convolution fusion | flops 136840704 | bytes 3674112 | tf_op jit(solution)/shard_map/hmt,the->mhe/dot_general | solution.py:44
  135.5 1.3 copy.34
  136.8 0.0 copy-done.4
  136.8 32.0 %while.10 = (s32[]{:T(128)}, f32[128,1024]{1,0:T(8,128)S(1)}, pred[]{:T(512)}, f32[1,1024]{1,0:T(1,128)S(1)}, f32[128,1024]{1,0:T(8,128)S(1)}, /*index=5*/f32[128,1024]{1,0:T(8,128)S(1)}, s32[]{:T(128)}) while((s32[]{:T(128)}, f32[128,1024]{1,0:T(8,128)S(1)}, pred[]{:T(512)}, f32[1,1024]{1,0:T(1,128)S(1)}, f32[128,1024]{1,0:T(8,128)S(1)}, ...), condition=%wide.region_3.4_spmd, body=%wide.region_2.3_spmd.sunk | while | flops 393218 | bytes 5247094 | solution.py:55
  136.8 0.1 multiply_add_fusion.2
  136.9 1.9 collective-permute-start
  138.8 8.6 %collective-permute-done = f32[128,1024]{1,0:T(8,128)S(1)} collective-permute-done((f32[128,1024]{1,0:T(8,128)S(1)}, f32[128,1024]{1,0:T(8,128)S(1)}, u32[]{:S(2)}, u32[]{:S(2)}) %collective-permute-start) | collective-permute-done | bytes 524320 | tf_op jit(solution)/shard_map/while/body/eval_jaxpr/ppermute | solution.py:12
  147.4 0.1 broadcast_select_fusion.2
  147.4 0.1 multiply_add_fusion.2
  147.5 1.9 collective-permute-start
  149.4 8.6 %collective-permute-done = f32[128,1024]{1,0:T(8,128)S(1)} collective-permute-done((f32[128,1024]{1,0:T(8,128)S(1)}, f32[128,1024]{1,0:T(8,128)S(1)}, u32[]{:S(2)}, u32[]{:S(2)}) %collective-permute-start) | collective-permute-done | bytes 524320 | tf_op jit(solution)/shard_map/while/body/eval_jaxpr/ppermute | solution.py:12
  158.0 0.1 broadcast_select_fusion.2
  158.1 0.1 multiply_add_fusion.2
  158.2 1.9 collective-permute-start
  160.1 8.6 %collective-permute-done = f32[128,1024]{1,0:T(8,128)S(1)} collective-permute-done((f32[128,1024]{1,0:T(8,128)S(1)}, f32[128,1024]{1,0:T(8,128)S(1)}, u32[]{:S(2)}, u32[]{:S(2)}) %collective-permute-start) | collective-permute-done | bytes 524320 | tf_op jit(solution)/shard_map/while/body/eval_jaxpr/ppermute | solution.py:12
  168.7 0.1 broadcast_select_fusion.2
  168.7 0.1 copy.49
  168.8 0.2 multiply_reduce_fusion.1
  169.1 0.1 copy.36
  169.2 0.2 multiply_convert_fusion
  169.5 37.6 %all-gather.7.cloned.1.call-done = bf16[2048,1024]{1,0:T(8,128)(2,1)} async-done(((bf16[512,1024]{1,0:T(8,128)(2,1)}), bf16[2048,1024]{1,0:T(8,128)(2,1)}) %all-gather.7.cloned.1.call-update) | async-done | bytes 4194320 | tf_op jit(solution)/shard_map/all_gather | solution.py:36
  207.0 5.2 %fusion.18 = bf16[64,8,8,128]{3,2,1,0:T(8,128)(2,1)S(1)} fusion(bf16[2048,1024]{1,0:T(8,128)(2,1)} %all-gather.7.cloned.1.call-done, bf16[1,512,2048]{2,1,0:T(8,128)(2,1)} %all-gather.9.cloned.1.call-done), kind=kOutput, calls=%fused_computation.21 | convolution fusion | flops 2148007936 | bytes 7340032 | tf_op jit(solution)/shard_map/dot_general | solution.py:22
  212.2 1.7 fusion.24
  213.9 1.3 fusion.63
  215.3 10.4 %fusion.32 = f32[8,128,512]{2,1,0:T(8,128)} fusion(f32[8,512]{1,0:T(8,128)S(1)} %fusion.63, bf16[128,8,128]{2,1,0:T(8,128)(2,1)S(1)} %bitcast_convert_fusion, f32[8,512,128]{2,1,0:T(8,128)} %fusion.24), kind=kOutput, calls=%fused_computation.31 | convolution fusion | flops 136319104 | bytes 4472832 | tf_op jit(solution)/shard_map/htm,mhe->the/dot_general | solution.py:66
  225.7 3.0 %copy.41 = f32[1,512,1024]{2,1,0:T(8,128)} copy(f32[1,512,1024]{1,2,0:T(8,128)} %bitcast.81) | data formatting | bytes 4194304 | tf_op jit(solution)/shard_map/reshape | solution.py:72
  228.7 0.0 copy-done.3
  228.7 2.9 %add_convert_fusion = bf16[1,512,1024]{2,1,0:T(8,128)(2,1)} fusion(f32[1,512,1024]{2,1,0:T(8,128)} %copy.41, bf16[1,512,1024]{2,1,0:T(8,128)(2,1)S(1)} %copy-done.3), kind=kLoop, calls=%fused_computation.12 | loop fusion | flops 1572864 | bytes 4194304 | tf_op jit(solution)/shard_map/convert_element_type | solution.py:72
  231.6 0.9 add_bitcast_fusion
  (5 shorter events, 0.1 us)
Async XLA Ops:
  7.2 124.2 %copy-start = (bf16[128,1024]{1,0:T(8,128)(2,1)S(1)}, bf16[128,1024]{1,0:T(8,128)(2,1)}, u32[]{:S(2)}) copy-start(bf16[128,1024]{1,0:T(8,128)(2,1)} %param.11) | copy-start | bytes 786436
  7.2 2.2 copy-start.2
  7.2 35.7 %all-gather.9.cloned.1.call-start = ((), (), s32[]{:S(2)}) async-start(), calls=%async_computation.2 | async-start | bytes 3145728 | tf_op jit(solution)/shard_map/all_gather | solution.py:30
  7.9 2.8 %copy-start.1 = (f32[1,128,1024]{2,1,0:T(8,128)S(1)}, f32[1,128,1024]{2,1,0:T(8,128)}, u32[]{:S(2)}) copy-start(f32[1,128,1024]{2,1,0:T(8,128)} %param.12) | copy-start | bytes 1572868
  7.9 118.3 %all-gather.5.cloned.1.call-start = ((), (), s32[]{:S(2)}) async-start(), calls=%async_computation | async-start | bytes 5242880 | tf_op jit(solution)/shard_map/all_gather | solution.py:35
  8.7 198.3 %all-gather.7.cloned.1.call-start = ((), (), s32[]{:S(2)}) async-start(), calls=%async_computation.1 | async-start | bytes 5242880 | tf_op jit(solution)/shard_map/all_gather | solution.py:36
  132.4 4.4 %copy-start.4 = (f32[1,1,1024]{2,1,0:T(1,128)S(1)}, f32[1,1,1024]{2,1,0:T(1,128)}, u32[]{:S(2)}) copy-start(f32[1,1,1024]{2,1,0:T(1,128)} %param.13) | copy-start | bytes 12292
  136.9 10.5 %collective-permute-start = (f32[128,1024]{1,0:T(8,128)S(1)}, f32[128,1024]{1,0:T(8,128)S(1)}, u32[]{:S(2)}, u32[]{:S(2)}) collective-permute-start(f32[128,1024]{1,0:T(8,128)S(1)} %multiply_add_fusion.2), channel_id=1, source_target_pairs={{0,8},{8,16},{16,24},{1,9},{9,17},{17,25},{2,10},{10,18},{18,26},{... | collective-permute-start | bytes 1572872 | tf_op jit(solution)/shard_map/while/body/eval_jaxpr/ppermute | solution.py:12
  147.5 10.5 %collective-permute-start = (f32[128,1024]{1,0:T(8,128)S(1)}, f32[128,1024]{1,0:T(8,128)S(1)}, u32[]{:S(2)}, u32[]{:S(2)}) collective-permute-start(f32[128,1024]{1,0:T(8,128)S(1)} %multiply_add_fusion.2), channel_id=1, source_target_pairs={{0,8},{8,16},{16,24},{1,9},{9,17},{17,25},{2,10},{10,18},{18,26},{... | collective-permute-start | bytes 1572872 | tf_op jit(solution)/shard_map/while/body/eval_jaxpr/ppermute | solution.py:12
  158.2 10.5 %collective-permute-start = (f32[128,1024]{1,0:T(8,128)S(1)}, f32[128,1024]{1,0:T(8,128)S(1)}, u32[]{:S(2)}, u32[]{:S(2)}) collective-permute-start(f32[128,1024]{1,0:T(8,128)S(1)} %multiply_add_fusion.2), channel_id=1, source_target_pairs={{0,8},{8,16},{16,24},{1,9},{9,17},{17,25},{2,10},{10,18},{18,26},{... | collective-permute-start | bytes 1572872 | tf_op jit(solution)/shard_map/while/body/eval_jaxpr/ppermute | solution.py:12
  225.7 3.0 %copy-start.3 = (bf16[1,512,1024]{2,1,0:T(8,128)(2,1)S(1)}, bf16[1,512,1024]{2,1,0:T(8,128)(2,1)}, u32[]{:S(2)}) copy-start(bf16[1,512,1024]{2,1,0:T(8,128)(2,1)} %param.8) | copy-start | bytes 3145732
Sparse Core Ops, SparseCore 0:
  9.5 33.3 all-gather.8
  44.5 81.6 all-gather.4
  127.8 79.2 all-gather.6
where the time goes:
time: 241 us; the launch traced here: 239 us
  waiting for transfers between devices  181 us (75%)
  matrix products  27.3 us (11%)
  between operations  13.9 us (6%)
  local copies, waits for them, and re-layouts  5.92 us (2%)
  starting transfers between devices  5.88 us (2%)
  other arithmetic  5.18 us (2%)
    all_gather x1, waiting for transfers between devices, shards(): keys_full = add_one(lax.all_gather(key_weight, 'vid', axis=0, tiled=True))  83.3 us
    all_gather x1, waiting for transfers between devices, shards(): lax.all_gather(query_weight, 'vid', axis=0, tiled=True)  37.6 us
    all_gather x1, waiting for transfers between devices, shards(): whole = lax.all_gather(local, 'tp', axis=1, tiled=True)  32.1 us
    ppermute x3, waiting for transfers between devices, from_behind(): return lax.ppermute(block, axis, route)  25.7 us
    dot_general x1, matrix products, shards(): jnp.einsum('htm,mhe->the', read_weights, grouped.astype(jnp.bfloat16), pr...  10.4 us
    dot_general x2, matrix products, add_rows(): return jnp.dot(left, piece, preferred_element_type=jnp.float32)  10.3 us
    ppermute x3, starting transfers between devices, from_behind(): return lax.ppermute(block, axis, route)  5.76 us
  transfers between devices with their start and end apart: 6, of which 6 were waited for; matrix products, arithmetic and copies ran while one was open for 5% of the time, Pallas kernels for 0%

commit v1 on v0

--- a/solution.py
+++ b/solution.py
@@ -1,6 +1,10 @@
+import functools
+
 import jax
 import jax.numpy as jnp
 from jax import lax
+from jax.experimental import pallas as pl
+from jax.experimental.pallas import tpu as pltpu
 from jax.sharding import PartitionSpec as P
 
 HEAD = 128
@@ -73,6 +77,339 @@
     return (mixed[None], memory_out[None])
 
 
+CORES = 2
+
+
+def softmax_rows(scores):
+    top = jnp.max(scores, axis=-1, keepdims=True)
+    expo = jnp.exp(scores - top)
+    return (expo * (1.0 / jnp.sum(expo, axis=-1, keepdims=True))).astype(jnp.bfloat16)
+
+
+def fused_kernel(
+    segs, vids, tps,
+    tokens, key_w, query_w, latent, init_memory, forget,
+    mixed, memory_out,
+    weights, tok, keys, queries, memory_in, update,
+    load_sem, tok_send, tok_recv, z_send, z_recv, y_send, y_recv, d_send, d_recv, m_send, m_recv,
+):
+    chips = segs // CORES
+    s, z, t = lax.axis_index("seg"), lax.axis_index("vid"), lax.axis_index("tp")
+    y, core = s // CORES, s % CORES
+    partner = y * CORES + (1 - core)
+    width = tokens.shape[1]
+    heads = width // HEAD
+    rows = weights.shape[2] * weights.shape[3]
+    sides = (1, -1)
+
+    def remote(src, dst, send, recv, device):
+        return pltpu.make_async_remote_copy(
+            src_ref=src, dst_ref=dst, send_sem=send, recv_sem=recv,
+            device_id=device, device_id_type=pl.DeviceIdType.MESH,
+        )
+
+    def z_copy(k, source, side):
+        block = weights.at[k, source, s]
+        return remote(block, block, z_send.at[k, source, (1 - side) // 2], z_recv.at[k, source], {"vid": z + side})
+
+    def y_copy(k, source, chip, side):
+        block = weights.at[k, source, chip * CORES + core]
+        return remote(
+            block, block, y_send.at[k, source, chip, (1 - side) // 2], y_recv.at[k, source, chip], {"seg": s + side * CORES}
+        )
+
+    def d_copy(k, source, chip, owner):
+        block = weights.at[k, source, chip * CORES + owner]
+        return remote(block, block, d_send.at[k, source, chip], d_recv.at[k, source, chip], {"seg": partner})
+
+    def m_copy(h):
+        cols = pl.ds(h * HEAD, HEAD)
+        return remote(memory_out.at[:, cols], memory_in.at[:, cols], m_send.at[h], m_recv.at[h], {"seg": s + 1})
+
+    def inside(index, size):
+        return (index >= 0) & (index < size)
+
+    def flag(condition):
+        return jnp.where(condition, 1, 0).astype(jnp.int32)
+
+    loads = [
+        pltpu.make_async_copy(key_w, weights.at[0, z], load_sem.at[0]),
+        pltpu.make_async_copy(tokens, tok.at[t], load_sem.at[1]),
+        pltpu.make_async_copy(query_w, weights.at[1, z], load_sem.at[2]),
+    ]
+    for load in loads:
+        load.start()
+    first_memory = pltpu.make_async_copy(init_memory, memory_in, load_sem.at[3])
+
+    @pl.when(s == 0)
+    def _():
+        first_memory.start()
+
+    barrier = pltpu.get_barrier_semaphore()
+    greeted = [
+        (z + 1 < vids, {"vid": z + 1}),
+        (z > 0, {"vid": z - 1}),
+        (y + 1 < chips, {"seg": s + CORES}),
+        (y > 0, {"seg": s - CORES}),
+        ((core == 1) & (y + 1 < chips), {"seg": s + 1}),
+        ((core == 0) & (y > 0), {"seg": s - 1}),
+        (s >= 0, {"seg": partner}),
+        (s >= 0, {"tp": 1 - t}),
+    ]
+    count = 0
+    for condition, device in greeted:
+        count = count + flag(condition)
+
+        @pl.when(condition)
+        def _(device=device):
+            pl.semaphore_signal(barrier, inc=1, device_id=device, device_id_type=pl.DeviceIdType.MESH)
+
+    pl.semaphore_wait(barrier, count)
+
+    def own_sends(k):
+        for side in sides:
+            @pl.when(inside(z + side, vids))
+            def _(side=side):
+                z_copy(k, z, side).start()
+
+    tok_copy = remote(tok.at[t], tok.at[t], tok_send, tok_recv, {"tp": 1 - t})
+    loads[0].wait()
+    own_sends(0)
+    loads[1].wait()
+    tok_copy.start()
+    loads[2].wait()
+
+    def each_source(distance, action):
+        for side in sides:
+            source = z - side * distance
+
+            @pl.when(inside(source, vids))
+            def _(source=source, side=side):
+                action(source, side)
+
+    def arrive_z(k, distance):
+        def action(source, side):
+            z_copy(k, source, side).wait_recv()
+
+            @pl.when(inside(z + side, vids))
+            def _():
+                z_copy(k, source, side).start()
+
+            for step in sides:
+                @pl.when(inside(y + step, chips))
+                def _(step=step):
+                    y_copy(k, source, y, step).start()
+
+            d_copy(k, source, y, core).start()
+
+        each_source(distance, action)
+
+    def each_chip(action):
+        for gap in range(1, chips):
+            for step in sides:
+                chip = y - step * gap
+
+                @pl.when(inside(chip, chips))
+                def _(chip=chip, step=step):
+                    action(chip, step)
+
+    def arrive_y(k, distance):
+        def action(source, side):
+            def one(chip, step):
+                y_copy(k, source, chip, step).wait_recv()
+
+                @pl.when(inside(y + step, chips))
+                def _():
+                    y_copy(k, source, chip, step).start()
+
+                d_copy(k, source, chip, core).start()
+
+            each_chip(one)
+
+        each_source(distance, action)
+
+    def arrive_d(k, distance):
+        def action(source, side):
+            for chip in range(chips):
+                d_copy(k, source, chip, 1 - core).wait_recv()
+
+        each_source(distance, action)
+
+    def project(k, out, begin, end):
+        tile = 2 * HEAD
+        for at in range(begin, end, tile):
+            total = None
+            for source in range(vids):
+                left = tok[source * rows // width, :, pl.ds(source * rows % width, rows)]
+                right = weights[k, source, :, :, pl.ds(at, tile)].reshape(rows, tile)
+                term = jnp.dot(left, right, preferred_element_type=jnp.float32)
+                total = term if total is None else total + term
+            out[:, pl.ds(at, tile)] = total.astype(jnp.bfloat16)
+
+    scale = 1.0 / jnp.sqrt(jnp.float32(HEAD))
+
+    def resample(h):
+        cols = pl.ds(h * HEAD, HEAD)
+        scores = lax.dot_general(
+            latent[:, cols], keys[:, cols], (((1,), (1,)), ((), ())), preferred_element_type=jnp.float32
+        )
+        update[:, cols] = jnp.dot(softmax_rows(scores * scale), tok[t, :, cols], preferred_element_type=jnp.float32)
+
+    def carry(h):
+        cols = pl.ds(h * HEAD, HEAD)
+
+        @pl.when(s > 0)
+        def _():
+            remote(
+                memory_out.at[:, cols], memory_in.at[:, cols], m_send.at[h], m_recv.at[h], {"seg": s - 1}
+            ).wait_recv()
+
+        memory_out[:, cols] = forget[:, cols] * memory_in[:, cols] + update[:, cols]
+
+        @pl.when(s + 1 < segs)
+        def _():
+            m_copy(h).start()
+
+    def readout(h):
+        cols = pl.ds(h * HEAD, HEAD)
+        held = memory_in[:, cols]
+        normed = held * lax.rsqrt(jnp.mean(held * held, axis=-1, keepdims=True) + 1e-06)
+        scores = lax.dot_general(
+            queries[:, cols], normed.astype(jnp.bfloat16), (((1,), (1,)), ((), ())), preferred_element_type=jnp.float32
+        )
+        read = jnp.dot(softmax_rows(scores * scale), held.astype(jnp.bfloat16), preferred_element_type=jnp.float32)
+        mixed[:, cols] = (tok[t, :, cols].astype(jnp.float32) + read).astype(jnp.bfloat16)
+
+    events = sorted(
+        [(distance, 0, distance) for distance in range(1, vids)]
+        + [(distance + 1.5, 1, distance) for distance in range(1, vids)]
+    )
+    last_key = max(i for i, (_, k, _) in enumerate(events) if k == 0)
+    for i, (_, k, distance) in enumerate(events[: last_key + 1]):
+        arrive_z(k, distance)
+        if i == 0:
+            own_sends(1)
+        else:
+            arrive_y(*events[i - 1][1:])
+    arrive_y(*events[last_key][1:])
+    later = events[last_key + 1 :]
+    arrive_z(*later[0][1:])
+    for distance in range(1, vids):
+        arrive_d(0, distance)
+    tok_arrival = remote(tok.at[1 - t], tok.at[1 - t], tok_send, tok_recv, {"tp": 1 - t})
+    tok_arrival.wait_recv()
+    project(0, keys, 0, width)
+    for i, event in enumerate(later[1:]):
+        arrive_y(*later[i][1:])
+        arrive_z(*event[1:])
+    for h in range(heads):
+        resample(h)
+
+    @pl.when(s == 0)
+    def _():
+        first_memory.wait()
+
+    for h in range(heads):
+        carry(h)
+    arrive_y(*later[-1][1:])
+    for distance in range(1, vids):
+        arrive_d(1, distance)
+    project(1, queries, 0, width)
+    for h in range(heads):
+        readout(h)
+
+    tok_copy.wait_send()
+    for k in range(2):
+        for side in sides:
+            @pl.when(inside(z + side, vids))
+            def _(k=k, side=side):
+                z_copy(k, z, side).wait_send()
+
+        for distance in range(1, vids):
+            def sent(source, side, k=k):
+                @pl.when(inside(z + side, vids))
+                def _():
+                    z_copy(k, source, side).wait_send()
+
+                for step in sides:
+                    @pl.when(inside(y + step, chips))
+                    def _(step=step):
+                        y_copy(k, source, y, step).wait_send()
+
+                d_copy(k, source, y, core).wait_send()
+
+                def one(chip, step):
+                    @pl.when(inside(y + step, chips))
+                    def _():
+                        y_copy(k, source, chip, step).wait_send()
+
+                    d_copy(k, source, chip, core).wait_send()
+
+                each_chip(one)
+
+            each_source(distance, sent)
+
+    @pl.when(s + 1 < segs)
+    def _():
+        for h in range(heads):
+            m_copy(h).wait_send()
+
+
+def fused_shards(sizes, tokens, key_weight, query_weight, latent_queries, init_memory, forget):
+    segs, vids, tps = sizes
+    local = tokens[0]
+    count, width = local.shape
+    latents = latent_queries.shape[0]
+    rows = key_weight.shape[0]
+    heads = width // HEAD
+    chips = segs // CORES
+    parts = (segs, rows // segs, width)
+    anywhere = pl.BlockSpec(memory_space=pl.ANY)
+    vmem = pl.BlockSpec(memory_space=pltpu.VMEM)
+    dma = pltpu.SemaphoreType.DMA
+    mixed, memory = pl.pallas_call(
+        functools.partial(fused_kernel, segs, vids, tps),
+        out_shape=(
+            jax.ShapeDtypeStruct((count, width), jnp.bfloat16),
+            jax.ShapeDtypeStruct((latents, width), jnp.float32),
+        ),
+        in_specs=[anywhere, anywhere, anywhere, vmem, anywhere, vmem],
+        out_specs=(vmem, vmem),
+        scratch_shapes=[
+            pltpu.VMEM((2, vids) + parts, jnp.bfloat16),
+            pltpu.VMEM((tps, count, width), jnp.bfloat16),
+            pltpu.VMEM((count, width), jnp.bfloat16),
+            pltpu.VMEM((count, width), jnp.bfloat16),
+            pltpu.VMEM((latents, width), jnp.float32),
+            pltpu.VMEM((latents, width), jnp.float32),
+            dma((4,)),
+            dma,
+            dma,
+            dma((2, vids, 2)),
+            dma((2, vids)),
+            dma((2, vids, chips, 2)),
+            dma((2, vids, chips)),
+            dma((2, vids, chips)),
+            dma((2, vids, chips)),
+            dma((heads,)),
+            dma((heads,)),
+        ],
+        compiler_params=pltpu.CompilerParams(collective_id=0, has_side_effects=True),
+    )(
+        local,
+        key_weight.reshape(parts),
+        query_weight.reshape(parts),
+        latent_queries,
+        init_memory[0],
+        forget[0],
+    )
+    return (mixed[None], memory[None])
+
+
+def relay_fits(segs, vids, tps):
+    return tps == 2 and segs % CORES == 0 and vids > 2 and segs * vids <= 32
+
+
 def solution(mesh):
     placed = (
         P("vid", "seg", "tp"),
@@ -82,8 +419,10 @@
         P("vid", None, "tp"),
         P("vid", "seg", "tp"),
     )
+    sizes = tuple(mesh.shape[axis] for axis in ("seg", "vid", "tp"))
+    body = functools.partial(fused_shards, sizes) if relay_fits(*sizes) else shards
     return jax.shard_map(
-        shards,
+        body,
         mesh=mesh,
         in_specs=placed,
         out_specs=(P("vid", "seg", "tp"), P("vid", "seg", "tp")),

time: 241 us -> 68.7 us (0.29)
  waiting for transfers between devices: 181 us -> 0 us
  Pallas kernels: 0 us -> 64.7 us
  matrix products: 27.3 us -> 0 us
  between operations: 13.9 us -> 0.65 us
  starting transfers between devices: 5.88 us -> 0 us
  other arithmetic: 5.18 us -> 0 us
  local copies, waits for them, and re-layouts: 5.92 us -> 3.12 us
    all_gather x3 -> x0, waiting for transfers between devices: 153 us -> none  [the longest x1 83.3 us: shards(): keys_full = add_one(lax.all_gather(key_weight, 'vid', axis=0, tiled=True))]
    pallas_call x0 -> x1, Pallas kernels: none -> 64.7 us  [fused_shards(): pl.pallas_call(functools.partial(fused_kernel, segs, vids, tps), out_shap...]
    dot_general x6 -> x0, matrix products: 26 us -> none  [the longest x1 10.4 us: shards(): jnp.einsum('htm,mhe->the', read_weights, grouped.astype(jnp.bfloat16), pr...]
    ppermute x3 -> x0, waiting for transfers between devices: 25.7 us -> none  [from_behind(): return lax.ppermute(block, axis, route)]
    ppermute x3 -> x0, starting transfers between devices: 5.76 us -> none  [from_behind(): return lax.ppermute(block, axis, route)]
    convert_element_type x3 -> x0, other arithmetic: 3.15 us -> none  [the longest x1 2.91 us: shards(): (local.astype(jnp.float32) + read.reshape(-1, width)).astype(jnp.bfloat16)]
    reshape x1 -> x0, local copies, waits for them, and re-layouts: 2.98 us -> none  [shards(): read.reshape(-1, width)]
    unnamed x12 -> x4, local copies, waits for them, and re-layouts: 0.16 us -> 3.12 us
  transfers between devices with their start and end apart: 6 -> 0, of which waited for: 6 -> 0; matrix products, arithmetic and copies ran while one was open for 5% -> 0% of each run, Pallas kernels for 0% -> 0%
where the time goes in v1:
time: 68.7 us; the launch traced here: 68.5 us
  Pallas kernels  64.7 us (94%)
  local copies, waits for them, and re-layouts  3.12 us (5%)
    pallas_call x1, Pallas kernels, fused_shards(): pl.pallas_call(functools.partial(fused_kernel, segs, vids, tps), out_shap...  64.7 us
    unnamed x4, local copies, waits for them, and re-layouts  3.12 us

profile of v1, /device:TPU:6, one launch (start us, length us, event | category | flops | bytes accessed | tf_op | source)
XLA Modules:
  0.0 68.5 jit_solution(9373123478265564027)
XLA Ops:
  0.6 64.7 %shard_map.77 = (bf16[512,1024]{1,0:T(8,128)(2,1)}, f32[128,1024]{1,0:T(8,128)}) custom-call(bf16[512,1024]{1,0:T(8,128)(2,1)} %bitcast.7, bf16[4,128,1024]{2,1,0:T(8,128)(2,1)} %bitcast.8, bf16[4,128,1024]{2,1,0:T(8,128)(2,1)} %bitcast.9, bf16[128,1024]{1,0:T(8,128)(2,1)} %latent.1, f32[128,1024]{1,0:T(8,128)} %bitcast.11, f32[1,1024]{1,0:T(1,128)} %bitcast.13), custom_call_target="tpu_custom_call" | custom-call | tf_op jit(solution)/shard_map/pallas_call | solution.py:370
  65.4 0.0 copy-start
  65.4 2.3 %copy.10 = bf16[1,512,1024]{2,1,0:T(8,128)(2,1)} copy(bf16[1,512,1024]{2,1,0:T(8,128)(2,1)} %bitcast.10) | data formatting | bytes 2097152
  67.7 0.0 copy-done
  67.7 0.8 %copy.11 = f32[1,128,1024]{2,1,0:T(8,128)} copy(f32[1,128,1024]{2,1,0:T(8,128)S(1)} %bitcast.12) | data formatting | bytes 1048576
Async XLA Ops:
  65.4 2.3 %copy-start = (f32[128,1024]{1,0:T(8,128)S(1)}, f32[128,1024]{1,0:T(8,128)}, u32[]{:S(2)}) copy-start(f32[128,1024]{1,0:T(8,128)} %get-tuple-element.5) | copy-start | bytes 1572868

commit v2 on v1

--- a/solution.py
+++ b/solution.py
@@ -77,6 +77,7 @@
     return (mixed[None], memory_out[None])
 
 
+SPLITS = 2
 CORES = 2
 
 
@@ -90,7 +91,7 @@
     segs, vids, tps,
     tokens, key_w, query_w, latent, init_memory, forget,
     mixed, memory_out,
-    weights, tok, keys, queries, memory_in, update,
+    weights, tok, keys, queries, memory_in, update, partial,
     load_sem, tok_send, tok_recv, z_send, z_recv, y_send, y_recv, d_send, d_recv, m_send, m_recv,
 ):
     chips = segs // CORES
@@ -100,6 +101,7 @@
     width = tokens.shape[1]
     heads = width // HEAD
     rows = weights.shape[2] * weights.shape[3]
+    streams = range(2 * SPLITS)
     sides = (1, -1)
 
     def remote(src, dst, send, recv, device):
@@ -132,14 +134,15 @@
     def flag(condition):
         return jnp.where(condition, 1, 0).astype(jnp.int32)
 
+    tok_load = pltpu.make_async_copy(tokens, tok.at[t], load_sem.at[0])
+    first_memory = pltpu.make_async_copy(init_memory, memory_in, load_sem.at[1])
     loads = [
-        pltpu.make_async_copy(key_w, weights.at[0, z], load_sem.at[0]),
-        pltpu.make_async_copy(tokens, tok.at[t], load_sem.at[1]),
-        pltpu.make_async_copy(query_w, weights.at[1, z], load_sem.at[2]),
+        pltpu.make_async_copy((key_w, query_w)[k // SPLITS].at[k % SPLITS], weights.at[k, z], load_sem.at[2 + k])
+        for k in streams
     ]
-    for load in loads:
+    key_streams, query_streams = streams[:SPLITS], streams[SPLITS:]
+    for load in loads[:SPLITS] + [tok_load] + loads[SPLITS:]:
         load.start()
-    first_memory = pltpu.make_async_copy(init_memory, memory_in, load_sem.at[3])
 
     @pl.when(s == 0)
     def _():
@@ -173,11 +176,13 @@
                 z_copy(k, z, side).start()
 
     tok_copy = remote(tok.at[t], tok.at[t], tok_send, tok_recv, {"tp": 1 - t})
-    loads[0].wait()
-    own_sends(0)
-    loads[1].wait()
+    for k in key_streams:
+        loads[k].wait()
+        own_sends(k)
+    tok_load.wait()
     tok_copy.start()
-    loads[2].wait()
+    for k in query_streams:
+        loads[k].wait()
 
     def each_source(distance, action):
         for side in sides:
@@ -228,23 +233,34 @@
 
         each_source(distance, action)
 
-    def arrive_d(k, distance):
+    last = jnp.where(2 * z < vids, vids - 1, 0)
+
+    def arrive_d(k, distance, final=None):
         def action(source, side):
-            for chip in range(chips):
-                d_copy(k, source, chip, 1 - core).wait_recv()
+            def take():
+                for chip in range(chips):
+                    d_copy(k, source, chip, 1 - core).wait_recv()
+
+            if final is None:
+                take()
+            else:
+                pl.when((source == last) == final)(take)
 
         each_source(distance, action)
 
-    def project(k, out, begin, end):
-        tile = 2 * HEAD
-        for at in range(begin, end, tile):
-            total = None
-            for source in range(vids):
-                left = tok[source * rows // width, :, pl.ds(source * rows % width, rows)]
-                right = weights[k, source, :, :, pl.ds(at, tile)].reshape(rows, tile)
+    tile = 2 * HEAD
+
+    def product(first, sources, at):
+        total = None
+        for source in sources:
+            begin = source * rows * SPLITS
+            for part in range(SPLITS):
+                place = pl.multiple_of(begin % width + part * rows, rows)
+                left = tok[begin // width, :, pl.ds(place, rows)]
+                right = weights[first + part, source, :, :, pl.ds(at, tile)].reshape(rows, tile)
                 term = jnp.dot(left, right, preferred_element_type=jnp.float32)
                 total = term if total is None else total + term
-            out[:, pl.ds(at, tile)] = total.astype(jnp.bfloat16)
+        return total
 
     scale = 1.0 / jnp.sqrt(jnp.float32(HEAD))
 
@@ -280,46 +296,74 @@
         read = jnp.dot(softmax_rows(scores * scale), held.astype(jnp.bfloat16), preferred_element_type=jnp.float32)
         mixed[:, cols] = (tok[t, :, cols].astype(jnp.float32) + read).astype(jnp.bfloat16)
 
-    events = sorted(
-        [(distance, 0, distance) for distance in range(1, vids)]
-        + [(distance + 1.5, 1, distance) for distance in range(1, vids)]
-    )
-    last_key = max(i for i, (_, k, _) in enumerate(events) if k == 0)
-    for i, (_, k, distance) in enumerate(events[: last_key + 1]):
-        arrive_z(k, distance)
-        if i == 0:
-            own_sends(1)
-        else:
-            arrive_y(*events[i - 1][1:])
-    arrive_y(*events[last_key][1:])
-    later = events[last_key + 1 :]
-    arrive_z(*later[0][1:])
+    def arrive_all_z(group, distance):
+        for k in group:
+            arrive_z(k, distance)
+
+    def arrive_all_y(group, distance):
+        for k in group:
+            arrive_y(k, distance)
+
     for distance in range(1, vids):
-        arrive_d(0, distance)
-    tok_arrival = remote(tok.at[1 - t], tok.at[1 - t], tok_send, tok_recv, {"tp": 1 - t})
-    tok_arrival.wait_recv()
-    project(0, keys, 0, width)
-    for i, event in enumerate(later[1:]):
-        arrive_y(*later[i][1:])
-        arrive_z(*event[1:])
-    for h in range(heads):
+        arrive_all_z(key_streams, distance)
+        if distance == vids - 2:
+            for k in query_streams:
+                own_sends(k)
+        if distance > 1:
+            arrive_all_y(key_streams, distance - 1)
+    arrive_all_y(key_streams, vids - 1)
+    arrive_all_z(query_streams, 1)
+    for distance in range(1, vids):
+        for k in key_streams:
+            arrive_d(k, distance)
+    remote(tok.at[1 - t], tok.at[1 - t], tok_send, tok_recv, {"tp": 1 - t}).wait_recv()
+    for at in range(0, width, tile):
+        keys[:, pl.ds(at, tile)] = product(0, range(vids), at).astype(jnp.bfloat16)
+    arrive_all_y(query_streams, 1)
+    for h in range(heads // 2):
+        resample(h)
+    for distance in range(2, vids - 1):
+        arrive_all_z(query_streams, distance)
+    for h in range(heads // 2, heads):
         resample(h)
 
     @pl.when(s == 0)
     def _():
         first_memory.wait()
 
-    for h in range(heads):
-        carry(h)
-    arrive_y(*later[-1][1:])
+    @pl.when(y == 0)
+    def _():
+        for h in range(heads):
+            carry(h)
+
+    for distance in range(2, vids - 1):
+        arrive_all_y(query_streams, distance)
+    arrive_all_z(query_streams, vids - 1)
+    for distance in range(1, vids - 1):
+        for k in query_streams:
+            arrive_d(k, distance, final=False)
+    others = [(last + 1 + i) % vids for i in range(vids - 1)]
+    for at in range(0, width, tile):
+        partial[:, pl.ds(at, tile)] = product(SPLITS, others, at)
+
+    @pl.when(y > 0)
+    def _():
+        for h in range(heads):
+            carry(h)
+
+    arrive_all_y(query_streams, vids - 1)
     for distance in range(1, vids):
-        arrive_d(1, distance)
-    project(1, queries, 0, width)
-    for h in range(heads):
-        readout(h)
+        for k in query_streams:
+            arrive_d(k, distance, final=True)
+    per_tile = tile // HEAD
+    for at in range(0, width, tile):
+        cols = pl.ds(at, tile)
+        queries[:, cols] = (partial[:, cols] + product(SPLITS, [last], at)).astype(jnp.bfloat16)
+        for h in range(at // HEAD, at // HEAD + per_tile):
+            readout(h)
 
     tok_copy.wait_send()
-    for k in range(2):
+    for k in streams:
         for side in sides:
             @pl.when(inside(z + side, vids))
             def _(k=k, side=side):
@@ -363,7 +407,8 @@
     rows = key_weight.shape[0]
     heads = width // HEAD
     chips = segs // CORES
-    parts = (segs, rows // segs, width)
+    parts = (segs, rows // segs // SPLITS, width)
+    streams = 2 * SPLITS
     anywhere = pl.BlockSpec(memory_space=pl.ANY)
     vmem = pl.BlockSpec(memory_space=pltpu.VMEM)
     dma = pltpu.SemaphoreType.DMA
@@ -376,29 +421,30 @@
         in_specs=[anywhere, anywhere, anywhere, vmem, anywhere, vmem],
         out_specs=(vmem, vmem),
         scratch_shapes=[
-            pltpu.VMEM((2, vids) + parts, jnp.bfloat16),
+            pltpu.VMEM((streams, vids) + parts, jnp.bfloat16),
             pltpu.VMEM((tps, count, width), jnp.bfloat16),
             pltpu.VMEM((count, width), jnp.bfloat16),
             pltpu.VMEM((count, width), jnp.bfloat16),
             pltpu.VMEM((latents, width), jnp.float32),
             pltpu.VMEM((latents, width), jnp.float32),
-            dma((4,)),
+            pltpu.VMEM((count, width), jnp.float32),
+            dma((2 + streams,)),
             dma,
             dma,
-            dma((2, vids, 2)),
-            dma((2, vids)),
-            dma((2, vids, chips, 2)),
-            dma((2, vids, chips)),
-            dma((2, vids, chips)),
-            dma((2, vids, chips)),
+            dma((streams, vids, 2)),
+            dma((streams, vids)),
+            dma((streams, vids, chips, 2)),
+            dma((streams, vids, chips)),
+            dma((streams, vids, chips)),
+            dma((streams, vids, chips)),
             dma((heads,)),
             dma((heads,)),
         ],
         compiler_params=pltpu.CompilerParams(collective_id=0, has_side_effects=True),
     )(
         local,
-        key_weight.reshape(parts),
-        query_weight.reshape(parts),
+        key_weight.reshape((SPLITS,) + parts),
+        query_weight.reshape((SPLITS,) + parts),
         latent_queries,
         init_memory[0],
         forget[0],

time: 68.7 us -> 64.2 us (0.934)
  Pallas kernels: 64.7 us -> 60.2 us
    pallas_call x1, Pallas kernels: 64.7 us -> 60.2 us  [fused_shards(): pl.pallas_call(functools.partial(fused_kernel, segs, vids, tps), out_shap...]
where the time goes in v2:
time: 64.2 us; the launch traced here: 64 us
  Pallas kernels  60.2 us (94%)
  local copies, waits for them, and re-layouts  3.12 us (5%)
  between operations  0.65 us (1%)
    pallas_call x1, Pallas kernels, fused_shards(): pl.pallas_call(functools.partial(fused_kernel, segs, vids, tps), out_shap...  60.2 us
    unnamed x4, local copies, waits for them, and re-layouts  3.12 us

profile of v2, /device:TPU:6, one launch (start us, length us, event | category | flops | bytes accessed | tf_op | source)
XLA Modules:
  0.0 64.0 jit_solution(14827951164756083901)
XLA Ops:
  0.6 60.2 %shard_map.77 = (bf16[512,1024]{1,0:T(8,128)(2,1)}, f32[128,1024]{1,0:T(8,128)}) custom-call(bf16[512,1024]{1,0:T(8,128)(2,1)} %bitcast.7, bf16[2,4,64,1024]{3,2,1,0:T(8,128)(2,1)} %bitcast.8, bf16[2,4,64,1024]{3,2,1,0:T(8,128)(2,1)} %bitcast.9, bf16[128,1024]{1,0:T(8,128)(2,1)} %latent.1, f32[128,1024]{1,0:T(8,128)} %bitcast.11, f32[1,1024]{1,0:T(1,128)} %bitcast.13), custom_call_target="tpu_custom_call" | custom-call | tf_op jit(solution)/shard_map/pallas_call | solution.py:415
  60.8 0.0 copy-start
  60.8 2.3 %copy.10 = bf16[1,512,1024]{2,1,0:T(8,128)(2,1)} copy(bf16[1,512,1024]{2,1,0:T(8,128)(2,1)} %bitcast.10) | data formatting | bytes 2097152
  63.2 0.0 copy-done
  63.2 0.8 %copy.11 = f32[1,128,1024]{2,1,0:T(8,128)} copy(f32[1,128,1024]{2,1,0:T(8,128)S(1)} %bitcast.12) | data formatting | bytes 1048576
Async XLA Ops:
  60.8 2.3 %copy-start = (f32[128,1024]{1,0:T(8,128)S(1)}, f32[128,1024]{1,0:T(8,128)}, u32[]{:S(2)}) copy-start(f32[128,1024]{1,0:T(8,128)} %get-tuple-element.5) | copy-start | bytes 1572868
